TPU v7x, 32 devices: a whole 2x2x4 slice. The times are simulated.
32 devices in a mesh: blk: 16 (over z, y, core), grp: 2 (over x).
Axes of the slice: x: 2, y: 2, z: 4, core: 2. Of those that a mesh axis runs over, the one named last changes fastest.
Arguments:
- layer_one: bfloat16 [1792, 1024], P(('blk', 'grp')), may hold values from -6 to 6
- layer_two: bfloat16 [1792, 1024], P(('blk', 'grp')), may hold values from -6 to 6
- spread: int32 [2], replicated, may hold values from 1024 to 4096
Outputs:
- profiles: float32 [2, 1792], P(None, ('blk', 'grp'))
- alignment: float32 [], replicated
All inputs are finite; a program needn't handle non-finite values.
Results may differ from a plain program's by a relative error of at most 0.0003.
Values may be sent and summed in bfloat16 or wider, within the bound.
A program may use at most 128 MiB of HBM per device.

v0:
```python
import jax
import jax.numpy as jnp
from jax import lax
from jax.sharding import PartitionSpec as P

D = 1024


def kernel_block(rows, sq_rows, cols, scale, offset):
    sq_cols = jnp.sum(cols.astype(jnp.float32) ** 2, axis=1)
    inner = lax.dot_general(
        rows, cols, (((1,), (1,)), ((), ())), preferred_element_type=jnp.float32
    )
    dist = sq_rows[:, None] + sq_cols[None, :] - 2.0 * inner
    return jnp.exp(-dist / (2.0 * scale)) - offset


def shards(layer_one, layer_two, spread):
    scales = spread.astype(jnp.float32)
    offsets = jnp.exp(-D / scales)
    stacked = jnp.stack([layer_one, layer_two])
    paired = lax.all_gather(stacked, "grp", axis=1, tiled=True)
    sq_pair = jnp.sum(paired.astype(jnp.float32) ** 2, axis=2)
    block = lax.all_gather(stacked, "blk", axis=1, tiled=True)
    first = kernel_block(paired[0], sq_pair[0], block[0], scales[0], offsets[0])
    second = kernel_block(paired[1], sq_pair[1], block[1], scales[1], offsets[1])
    first, second = (first, second)
    rows_acc = jnp.stack([jnp.sum(first, axis=1), jnp.sum(second, axis=1)])
    prods = jnp.stack([jnp.sum(first * second), jnp.sum(first * first), jnp.sum(second * second)])
    rows_acc, prods = (rows_acc, prods)
    own_rows = lax.psum_scatter(rows_acc, "grp", scatter_dimension=1, tiled=True)
    total = own_rows.shape[1] * lax.axis_size("blk") * lax.axis_size("grp")
    row_terms = jnp.stack(
        [
            jnp.sum(own_rows[0]),
            jnp.sum(own_rows[1]),
            jnp.sum(own_rows[0] * own_rows[1]),
            jnp.sum(own_rows[0] * own_rows[0]),
            jnp.sum(own_rows[1] * own_rows[1]),
        ]
    )
    prods = lax.psum(prods, ("blk", "grp"))
    row_terms = lax.psum(row_terms, ("blk", "grp"))
    sum_one, sum_two = (row_terms[0], row_terms[1])
    c_cross, c_one, c_two = (row_terms[2], row_terms[3], row_terms[4])
    h_cross = prods[0] - 2.0 * c_cross / total + sum_one * sum_two / (total * total)
    h_one = prods[1] - 2.0 * c_one / total + sum_one * sum_one / (total * total)
    h_two = prods[2] - 2.0 * c_two / total + sum_two * sum_two / (total * total)
    alignment = h_cross / jnp.sqrt(h_one * h_two)
    profiles = jnp.stack(
        [own_rows[0] / jnp.sqrt(c_one / total), own_rows[1] / jnp.sqrt(c_two / total)]
    )
    return (profiles, alignment)


def solution(mesh):
    return jax.shard_map(
        shards,
        mesh=mesh,
        in_specs=(P(("blk", "grp"), None), P(("blk", "grp"), None), P()),
        out_specs=(P(None, ("blk", "grp")), P()),
        check_vma=False,
    )
```

profile of v0, /device:TPU:0, one launch (start us, length us, event | category | flops | bytes accessed | tf_op | source)
XLA Modules:
  0.0 135.6 jit_solution(13423032327136159622)
XLA Ops:
  7.2 0.0 all-gather.2.cloned.1.call-start
  7.2 1.7 %pad_maximum_fusion = bf16[2,56,1024]{2,1,0:T(8,128)(2,1)} fusion(bf16[1,56,1024]{2,1,0:T(8,128)(2,1)} %bitcast.70, bf16[1,56,1024]{2,1,0:T(8,128)(2,1)} %bitcast.71), kind=kLoop, calls=%fused_computation.24 | loop fusion | flops 114688 | bytes 458752 | tf_op jit(solution)/shard_map/stack | solution.py:21
  8.9 0.0 all-gather.2.cloned.1.call-update
  8.9 0.7 convert_element_type.14
  9.6 0.6 fusion.16
  11.5 1.2 dynamic-slice
  13.4 0.7 divide_exponential_fusion
  14.0 0.6 fusion.17
  14.6 9.5 %all_gather.6 = bf16[2,112,1024]{2,1,0:T(8,128)(2,1)S(1)} all-gather(bf16[2,56,1024]{2,1,0:T(8,128)(2,1)} %pad_maximum_fusion), channel_id=1, replica_groups=mesh['blk'=16,'grp'=2] {'grp'}, dimensions={1}, use_global_device_ids=true | all-gather | bytes 688128 | tf_op jit(solution)/shard_map/all_gather | solution.py:22
  24.1 0.2 multiply_reduce_fusion.2
  24.3 36.4 %all-gather.2.cloned.1.call-done = bf16[2,896,1024]{2,1,0:T(8,128)(2,1)} async-done(((bf16[2,56,1024]{2,1,0:T(8,128)(2,1)}), bf16[2,896,1024]{2,1,0:T(8,128)(2,1)}) %all-gather.2.cloned.1.call-update) | async-done | bytes 3670032 | tf_op jit(solution)/shard_map/all_gather | solution.py:24
  60.7 0.0 copy-start
  60.7 3.0 %multiply_reduce_fusion.1 = (f32[896]{0:T(1024)S(1)}, f32[896]{0:T(1024)S(1)}) fusion(bf16[2,896,1024]{2,1,0:T(8,128)(2,1)} %all-gather.2.cloned.1.call-done), kind=kLoop, calls=%fused_computation.1 | loop fusion | flops 5503232 | bytes 3677184 | tf_op jit(solution)/shard_map/reduce_sum | solution.py:10
  63.7 0.2 copy-done
  63.8 1.4 %fusion.10 = f32[112,896]{1,0:T(8,128)S(1)} fusion(bf16[2,896,1024]{2,1,0:T(8,128)(2,1)S(1)} %copy-done, bf16[2,112,1024]{2,1,0:T(8,128)(2,1)S(1)} %all_gather.6, f32[]{:T(128)} %bitcast.12, f32[]{:T(128)} %bitcast.11, f32[896]{0:T(1024)S(1)} %get-tuple-element.3, f32[112]{0:T(128)S(1)} %get-tuple-element.18), kind=kOutput, calls=%fused_computation.14 | convolution fusion | flops 206123008 | bytes 2470408 | tf_op jit(solution)/shard_map/dot_general | solution.py:11
  65.2 2.1 %multiply_reduce_fusion.5 = (f32[]{:T(128)}, f32[]{:T(128)}, f32[112]{0:T(128)S(1)}, f32[]{:T(128)}, f32[112]{0:T(128)S(1)}) fusion(f32[112,896]{1,0:T(8,128)S(1)} %fusion.10, f32[]{:T(128)} %bitcast.6, f32[]{:T(128)} %bitcast.5, bf16[2,896,1024]{2,1,0:T(8,128)(2,1)S(1)} %copy-done, bf16[2,112,1024]{2,1,0:T(8,128)(2,1)S(1)} %all_gather.6, ...), kind=kOutput, calls=%fused_computation.21 | convolution fusion | flops 206925600 | bytes 2471316 | tf_op jit(solution)/shard_map/dot_general | solution.py:11
  67.4 4.9 %all-reduce = f32[2,112]{1,0:T(2,128)S(1)} all-reduce(f32[2,112]{1,0:T(2,128)S(1)} %pad_maximum_fusion.1), channel_id=2, replica_groups=mesh['blk'=16,'grp'=2] {'grp'}, use_global_device_ids=true, to_apply=%region_5.0.clone | all-reduce | flops 224 | bytes 1792
  72.3 0.1 constant_dynamic-slice_fusion
  72.4 0.7 multiply_reduce_fusion.6
  73.0 2.0 %pad_maximum_fusion.3 = f32[3]{0:T(128)S(1)} fusion(f32[1]{0:T(128)} %bitcast.23, f32[1]{0:T(128)} %bitcast.22, f32[1]{0:T(128)} %bitcast.21), kind=kLoop, calls=%fused_computation.27 | loop fusion | flops 6 | bytes 24 | tf_op jit(solution)/shard_map/stack | solution.py:29
  75.0 3.2 %stack.64 = f32[5]{0:T(128)S(1)} concatenate(f32[1]{0:T(128)} %bitcast.14, f32[1]{0:T(128)} %bitcast.15, f32[1]{0:T(128)} %bitcast.16, f32[1]{0:T(128)} %bitcast.17, f32[1]{0:T(128)} %bitcast.18), dimensions={0} | concatenate | bytes 40 | tf_op jit(solution)/shard_map/stack | solution.py:33
  78.2 39.4 %all-reduce.1 = (f32[5]{0:T(128)S(1)}, f32[3]{0:T(128)S(1)}) all-reduce(f32[5]{0:T(128)S(1)} %stack.64, f32[3]{0:T(128)S(1)} %pad_maximum_fusion.3), channel_id=1, replica_groups=mesh['blk'=16,'grp'=2] {'blk','grp'}, use_global_device_ids=true, to_apply=%region_11.0 | all-reduce | flops 8 | bytes 64 | tf_op jit(solution)/shard_map/psum | solution.py:43
  117.6 0.7 fusion.14
  127.1 0.6 pad_maximum_fusion.2
  (3 shorter events, 0.0 us)
Async XLA Ops:
  7.2 53.5 %all-gather.2.cloned.1.call-start = ((), (), s32[]{:S(2)}) async-start(), calls=%async_computation | async-start | bytes 3899392 | tf_op jit(solution)/shard_map/all_gather | solution.py:24
  60.7 3.1 %copy-start = (bf16[2,896,1024]{2,1,0:T(8,128)(2,1)S(1)}, bf16[2,896,1024]{2,1,0:T(8,128)(2,1)}, u32[]{:S(2)}) copy-start(bf16[2,896,1024]{2,1,0:T(8,128)(2,1)} %all-gather.2.cloned.1.call-done) | copy-start | bytes 11010052
Sparse Core Ops, SparseCore 0:
  10.3 50.3 all-gather.1
where the time goes:
time: 136 us
  blocking collectives  53.8 us (40%)
  waiting for transfers between devices  36.4 us (27%)
  between operations  26 us (19%)
  other arithmetic  9.38 us (7%)
  local copies, waits for them, and re-layouts  6.55 us (5%)
  matrix products  3.5 us (3%)
    psum x1, blocking collectives, shards(): row_terms = lax.psum(row_terms, ('blk', 'grp'))  39.4 us
    all_gather x1, waiting for transfers between devices, shards(): block = lax.all_gather(stacked, 'blk', axis=1, tiled=True)  36.4 us
    all_gather x1, blocking collectives, shards(): paired = lax.all_gather(stacked, 'grp', axis=1, tiled=True)  9.49 us
    unnamed x1, blocking collectives  4.91 us
    dot_general x2, matrix products, kernel_block(): lax.dot_general(rows, cols, (((1,), (1,)), ((), ())), preferred_element_t...  3.5 us
    another operation x1, local copies, waits for them, and re-layouts, shards(): jnp.stack([jnp.sum(own_rows[0]), jnp.sum(own_rows[1]), jnp.sum(own_rows[0...  3.22 us
    reduce_sum x1, other arithmetic, kernel_block(): sq_cols = jnp.sum(cols.astype(jnp.float32) ** 2, axis=1)  2.99 us
  transfers between devices with their start and end apart: 1, of which 1 were waited for; matrix products, arithmetic and copies ran while one was open for 3% of the time, Pallas kernels for 0%

commit v1 on v0

--- a/solution.py
+++ b/solution.py
@@ -21,7 +21,12 @@
     stacked = jnp.stack([layer_one, layer_two])
     paired = lax.all_gather(stacked, "grp", axis=1, tiled=True)
     sq_pair = jnp.sum(paired.astype(jnp.float32) ** 2, axis=2)
-    block = lax.all_gather(stacked, "blk", axis=1, tiled=True)
+    ring = [stacked]
+    for hop in range(15):
+        ring.append(lax.ppermute(ring[-1], "blk", [(dev, (dev + 1) % 16) for dev in range(16)]))
+    block = jnp.roll(
+        jnp.concatenate(ring[::-1], axis=1), (lax.axis_index("blk") + 1) * ring[0].shape[1], axis=1
+    )
     first = kernel_block(paired[0], sq_pair[0], block[0], scales[0], offsets[0])
     second = kernel_block(paired[1], sq_pair[1], block[1], scales[1], offsets[1])
     first, second = (first, second)

time: 136 us -> 197 us (1.45)
  waiting for transfers between devices: 36.4 us -> 110 us
  between operations: 26 us -> 12.8 us
  local copies, waits for them, and re-layouts: 6.55 us -> 12.3 us
  blocking collectives: 53.8 us -> 48.4 us
  other arithmetic: 9.38 us -> 7.06 us
    ppermute x0 -> x15, waiting for transfers between devices: none -> 110 us  [shards(): lax.ppermute(ring[-1], 'blk', [(dev, (dev + 1) % 16) for dev in range(16)])]
    all_gather x1 -> x0, waiting for transfers between devices: 36.4 us -> none  [shards(): block = lax.all_gather(stacked, 'blk', axis=1, tiled=True)]
    unnamed x4 -> x40, local copies, waits for them, and re-layouts: 1.47 us -> 7.25 us
    all_gather x1, blocking collectives: 9.49 us -> 6.68 us  [shards(): paired = lax.all_gather(stacked, 'grp', axis=1, tiled=True)]
    psum x1, blocking collectives: 39.4 us -> 36.8 us  [shards(): row_terms = lax.psum(row_terms, ('blk', 'grp'))]
  transfers between devices with their start and end apart: 1 -> 15, of which waited for: 1 -> 15; matrix products, arithmetic and copies ran while one was open for 3% -> 2% of each run, Pallas kernels for 0% -> 0%
where the time goes in v1:
time: 197 us; the launch traced here: 195 us
  waiting for transfers between devices  110 us (56%)
  blocking collectives  48.4 us (25%)
  between operations  12.8 us (6%)
  local copies, waits for them, and re-layouts  12.3 us (6%)
  other arithmetic  7.06 us (4%)
  matrix products  3.51 us (2%)
    ppermute x15, waiting for transfers between devices, shards(): lax.ppermute(ring[-1], 'blk', [(dev, (dev + 1) % 16) for dev in range(16)])  110 us
    psum x1, blocking collectives, shards(): row_terms = lax.psum(row_terms, ('blk', 'grp'))  36.8 us
    unnamed x40, local copies, waits for them, and re-layouts  7.25 us
    all_gather x1, blocking collectives, shards(): paired = lax.all_gather(stacked, 'grp', axis=1, tiled=True)  6.68 us
    unnamed x1, blocking collectives  4.91 us
  transfers between devices with their start and end apart: 15, of which 15 were waited for; matrix products, arithmetic and copies ran while one was open for 2% of the time, Pallas kernels for 0%

profile of v1, /device:TPU:0, one launch (start us, length us, event | category | flops | bytes accessed | tf_op | source)
XLA Modules:
  0.0 195.2 jit_solution(2756869121061232474)
XLA Ops:
  0.6 1.0 pad_maximum_fusion
  2.2 8.7 %collective-permute-done = bf16[2,56,1024]{2,1,0:T(8,128)(2,1)S(1)} collective-permute-done((bf16[2,56,1024]{2,1,0:T(8,128)(2,1)S(1)}, bf16[2,56,1024]{2,1,0:T(8,128)(2,1)S(1)}, u32[]{:S(2)}, u32[]{:S(2)}) %collective-permute-start) | collective-permute-done | bytes 229408 | tf_op jit(solution)/shard_map/ppermute | solution.py:26
  10.9 8.1 %collective-permute-done.1 = bf16[2,56,1024]{2,1,0:T(8,128)(2,1)S(1)} collective-permute-done((bf16[2,56,1024]{2,1,0:T(8,128)(2,1)S(1)}, bf16[2,56,1024]{2,1,0:T(8,128)(2,1)S(1)}, u32[]{:S(2)}, u32[]{:S(2)}) %collective-permute-start.1) | collective-permute-done | bytes 229408 | tf_op jit(solution)/shard_map/ppermute | solution.py:26
  19.0 8.1 %collective-permute-done.2 = bf16[2,56,1024]{2,1,0:T(8,128)(2,1)S(1)} collective-permute-done((bf16[2,56,1024]{2,1,0:T(8,128)(2,1)S(1)}, bf16[2,56,1024]{2,1,0:T(8,128)(2,1)S(1)}, u32[]{:S(2)}, u32[]{:S(2)}) %collective-permute-start.2) | collective-permute-done | bytes 229408 | tf_op jit(solution)/shard_map/ppermute | solution.py:26
  27.2 8.1 %collective-permute-done.3 = bf16[2,56,1024]{2,1,0:T(8,128)(2,1)S(1)} collective-permute-done((bf16[2,56,1024]{2,1,0:T(8,128)(2,1)S(1)}, bf16[2,56,1024]{2,1,0:T(8,128)(2,1)S(1)}, u32[]{:S(2)}, u32[]{:S(2)}) %collective-permute-start.3) | collective-permute-done | bytes 229408 | tf_op jit(solution)/shard_map/ppermute | solution.py:26
  35.3 8.1 %collective-permute-done.4 = bf16[2,56,1024]{2,1,0:T(8,128)(2,1)S(1)} collective-permute-done((bf16[2,56,1024]{2,1,0:T(8,128)(2,1)S(1)}, bf16[2,56,1024]{2,1,0:T(8,128)(2,1)S(1)}, u32[]{:S(2)}, u32[]{:S(2)}) %collective-permute-start.4) | collective-permute-done | bytes 229408 | tf_op jit(solution)/shard_map/ppermute | solution.py:26
  43.5 8.1 %collective-permute-done.5 = bf16[2,56,1024]{2,1,0:T(8,128)(2,1)S(1)} collective-permute-done((bf16[2,56,1024]{2,1,0:T(8,128)(2,1)S(1)}, bf16[2,56,1024]{2,1,0:T(8,128)(2,1)S(1)}, u32[]{:S(2)}, u32[]{:S(2)}) %collective-permute-start.5) | collective-permute-done | bytes 229408 | tf_op jit(solution)/shard_map/ppermute | solution.py:26
  51.6 8.1 %collective-permute-done.6 = bf16[2,56,1024]{2,1,0:T(8,128)(2,1)S(1)} collective-permute-done((bf16[2,56,1024]{2,1,0:T(8,128)(2,1)S(1)}, bf16[2,56,1024]{2,1,0:T(8,128)(2,1)S(1)}, u32[]{:S(2)}, u32[]{:S(2)}) %collective-permute-start.6) | collective-permute-done | bytes 229408 | tf_op jit(solution)/shard_map/ppermute | solution.py:26
  59.8 8.1 %collective-permute-done.7 = bf16[2,56,1024]{2,1,0:T(8,128)(2,1)S(1)} collective-permute-done((bf16[2,56,1024]{2,1,0:T(8,128)(2,1)S(1)}, bf16[2,56,1024]{2,1,0:T(8,128)(2,1)S(1)}, u32[]{:S(2)}, u32[]{:S(2)}) %collective-permute-start.7) | collective-permute-done | bytes 229408 | tf_op jit(solution)/shard_map/ppermute | solution.py:26
  67.9 8.1 %collective-permute-done.8 = bf16[2,56,1024]{2,1,0:T(8,128)(2,1)S(1)} collective-permute-done((bf16[2,56,1024]{2,1,0:T(8,128)(2,1)S(1)}, bf16[2,56,1024]{2,1,0:T(8,128)(2,1)S(1)}, u32[]{:S(2)}, u32[]{:S(2)}) %collective-permute-start.8) | collective-permute-done | bytes 229408 | tf_op jit(solution)/shard_map/ppermute | solution.py:26
  76.1 8.1 %collective-permute-done.9 = bf16[2,56,1024]{2,1,0:T(8,128)(2,1)S(1)} collective-permute-done((bf16[2,56,1024]{2,1,0:T(8,128)(2,1)S(1)}, bf16[2,56,1024]{2,1,0:T(8,128)(2,1)S(1)}, u32[]{:S(2)}, u32[]{:S(2)}) %collective-permute-start.9) | collective-permute-done | bytes 229408 | tf_op jit(solution)/shard_map/ppermute | solution.py:26
  84.2 8.1 %collective-permute-done.10 = bf16[2,56,1024]{2,1,0:T(8,128)(2,1)S(1)} collective-permute-done((bf16[2,56,1024]{2,1,0:T(8,128)(2,1)S(1)}, bf16[2,56,1024]{2,1,0:T(8,128)(2,1)S(1)}, u32[]{:S(2)}, u32[]{:S(2)}) %collective-permute-start.10) | collective-permute-done | bytes 229408 | tf_op jit(solution)/shard_map/ppermute | solution.py:26
  93.0 7.5 %collective-permute-done.11 = bf16[2,56,1024]{2,1,0:T(8,128)(2,1)S(1)} collective-permute-done((bf16[2,56,1024]{2,1,0:T(8,128)(2,1)S(1)}, bf16[2,56,1024]{2,1,0:T(8,128)(2,1)S(1)}, u32[]{:S(2)}, u32[]{:S(2)}) %collective-permute-start.11) | collective-permute-done | bytes 229408 | tf_op jit(solution)/shard_map/ppermute | solution.py:26
  100.5 6.7 %all_gather.3 = bf16[2,112,1024]{2,1,0:T(8,128)(2,1)S(1)} all-gather(bf16[2,56,1024]{2,1,0:T(8,128)(2,1)S(1)} %pad_maximum_fusion), channel_id=1, replica_groups=mesh['blk'=16,'grp'=2] {'grp'}, dimensions={1}, use_global_device_ids=true | all-gather | bytes 688128 | tf_op jit(solution)/shard_map/all_gather | solution.py:22
  107.3 1.3 collective-permute-done.12
  110.6 7.0 %collective-permute-done.13 = bf16[2,56,1024]{2,1,0:T(8,128)(2,1)} collective-permute-done((bf16[2,56,1024]{2,1,0:T(8,128)(2,1)S(1)}, bf16[2,56,1024]{2,1,0:T(8,128)(2,1)}, u32[]{:S(2)}, u32[]{:S(2)}) %collective-permute-start.13) | collective-permute-done | bytes 229408 | tf_op jit(solution)/shard_map/ppermute | solution.py:26
  119.4 1.3 dynamic-slice
  121.3 4.7 %collective-permute-done.14 = bf16[2,56,1024]{2,1,0:T(8,128)(2,1)} collective-permute-done((bf16[2,56,1024]{2,1,0:T(8,128)(2,1)}, bf16[2,56,1024]{2,1,0:T(8,128)(2,1)}, u32[]{:S(2)}, u32[]{:S(2)}) %collective-permute-start.14) | collective-permute-done | bytes 229408 | tf_op jit(solution)/shard_map/ppermute | solution.py:26
  126.0 1.0 constant_dynamic-update-slice_fusion.31
  127.0 1.0 constant_dynamic-update-slice_fusion.30
  127.9 1.0 constant_dynamic-update-slice_fusion.29
  129.2 1.0 constant_dynamic-update-slice_fusion.15
  130.2 1.0 constant_dynamic-update-slice_fusion.14
  131.5 1.3 multiply_reduce_fusion.1
  132.8 1.4 exponential_subtract_fusion
  134.2 2.1 %multiply_reduce_fusion.5 = (f32[]{:T(128)}, f32[]{:T(128)}, f32[112]{0:T(128)S(1)}, f32[]{:T(128)}, f32[112]{0:T(128)S(1)}) fusion(f32[112,896]{1,0:T(8,128)S(1)} %exponential_subtract_fusion, f32[]{:T(128)} %bitcast.6, f32[]{:T(128)} %bitcast.5, bf16[2,1792,1024]{2,1,0:T(8,128)(2,1)S(1)} %constant_dynamic-update-slice_fusion, s32[]{:T(128)S(6)} %select_n.14, ...), kind=kOutput, calls=%fused_computation.11 | convolution fusion | flops 206925600 | bytes 2471320 | tf_op jit(solution)/shard_map/dot_general | solution.py:11
  136.3 4.9 %all-reduce = f32[2,112]{1,0:T(2,128)S(1)} all-reduce(f32[2,112]{1,0:T(2,128)S(1)} %pad_maximum_fusion.1), channel_id=2, replica_groups=mesh['blk'=16,'grp'=2] {'grp'}, use_global_device_ids=true, to_apply=%region_5.6.clone | all-reduce | flops 224 | bytes 1792
  141.3 0.7 multiply_reduce_fusion.6
  142.0 2.0 %pad_maximum_fusion.3 = f32[3]{0:T(128)S(1)} fusion(f32[1]{0:T(128)} %bitcast.23, f32[1]{0:T(128)} %bitcast.22, f32[1]{0:T(128)} %bitcast.21), kind=kLoop, calls=%fused_computation.51 | loop fusion | flops 6 | bytes 24 | tf_op jit(solution)/shard_map/stack | solution.py:34
  144.0 3.2 %stack.64 = f32[5]{0:T(128)S(1)} concatenate(f32[1]{0:T(128)} %bitcast.14, f32[1]{0:T(128)} %bitcast.15, f32[1]{0:T(128)} %bitcast.16, f32[1]{0:T(128)} %bitcast.17, f32[1]{0:T(128)} %bitcast.18), dimensions={0} | concatenate | bytes 40 | tf_op jit(solution)/shard_map/stack | solution.py:38
  147.2 36.8 %all-reduce.1 = (f32[5]{0:T(128)S(1)}, f32[3]{0:T(128)S(1)}) all-reduce(f32[5]{0:T(128)S(1)} %stack.64, f32[3]{0:T(128)S(1)} %pad_maximum_fusion.3), channel_id=1, replica_groups=mesh['blk'=16,'grp'=2] {'blk','grp'}, use_global_device_ids=true, to_apply=%region_11.12 | all-reduce | flops 8 | bytes 64 | tf_op jit(solution)/shard_map/psum | solution.py:48
  184.0 0.7 fusion.6
  (60 shorter events, 5.1 us)
Async XLA Ops:
  0.6 128.6 %copy-start.1 = (bf16[56,1024]{1,0:T(8,128)(2,1)S(1)}, bf16[56,1024]{1,0:T(8,128)(2,1)}, u32[]{:S(2)}) copy-start(bf16[56,1024]{1,0:T(8,128)(2,1)} %param.3) | copy-start | bytes 344068
  0.6 128.6 %copy-start = (bf16[56,1024]{1,0:T(8,128)(2,1)S(1)}, bf16[56,1024]{1,0:T(8,128)(2,1)}, u32[]{:S(2)}) copy-start(bf16[56,1024]{1,0:T(8,128)(2,1)} %param.4) | copy-start | bytes 344068
  1.7 9.2 %collective-permute-start = (bf16[2,56,1024]{2,1,0:T(8,128)(2,1)S(1)}, bf16[2,56,1024]{2,1,0:T(8,128)(2,1)S(1)}, u32[]{:S(2)}, u32[]{:S(2)}) collective-permute-start(bf16[2,56,1024]{2,1,0:T(8,128)(2,1)S(1)} %pad_maximum_fusion), channel_id=1, source_target_pairs={{0,2},{2,4},{4,6},{6,8},{8,10},{10,12},{12,14},{14,16},{16,18},{18... | collective-permute-start | bytes 688136 | tf_op jit(solution)/shard_map/ppermute | solution.py:26
  10.9 8.1 %collective-permute-start.1 = (bf16[2,56,1024]{2,1,0:T(8,128)(2,1)S(1)}, bf16[2,56,1024]{2,1,0:T(8,128)(2,1)S(1)}, u32[]{:S(2)}, u32[]{:S(2)}) collective-permute-start(bf16[2,56,1024]{2,1,0:T(8,128)(2,1)S(1)} %collective-permute-done), channel_id=1, source_target_pairs={{0,2},{2,4},{4,6},{6,8},{8,10},{10,12},{12,14},{14,16},{16,18},{18... | collective-permute-start | bytes 688136 | tf_op jit(solution)/shard_map/ppermute | solution.py:26
  19.0 8.1 %collective-permute-start.2 = (bf16[2,56,1024]{2,1,0:T(8,128)(2,1)S(1)}, bf16[2,56,1024]{2,1,0:T(8,128)(2,1)S(1)}, u32[]{:S(2)}, u32[]{:S(2)}) collective-permute-start(bf16[2,56,1024]{2,1,0:T(8,128)(2,1)S(1)} %collective-permute-done.1), channel_id=1, source_target_pairs={{0,2},{2,4},{4,6},{6,8},{8,10},{10,12},{12,14},{14,16},{16,18},{18... | collective-permute-start | bytes 688136 | tf_op jit(solution)/shard_map/ppermute | solution.py:26
  27.2 8.1 %collective-permute-start.3 = (bf16[2,56,1024]{2,1,0:T(8,128)(2,1)S(1)}, bf16[2,56,1024]{2,1,0:T(8,128)(2,1)S(1)}, u32[]{:S(2)}, u32[]{:S(2)}) collective-permute-start(bf16[2,56,1024]{2,1,0:T(8,128)(2,1)S(1)} %collective-permute-done.2), channel_id=1, source_target_pairs={{0,2},{2,4},{4,6},{6,8},{8,10},{10,12},{12,14},{14,16},{16,18},{18... | collective-permute-start | bytes 688136 | tf_op jit(solution)/shard_map/ppermute | solution.py:26
  35.3 8.1 %collective-permute-start.4 = (bf16[2,56,1024]{2,1,0:T(8,128)(2,1)S(1)}, bf16[2,56,1024]{2,1,0:T(8,128)(2,1)S(1)}, u32[]{:S(2)}, u32[]{:S(2)}) collective-permute-start(bf16[2,56,1024]{2,1,0:T(8,128)(2,1)S(1)} %collective-permute-done.3), channel_id=1, source_target_pairs={{0,2},{2,4},{4,6},{6,8},{8,10},{10,12},{12,14},{14,16},{16,18},{18... | collective-permute-start | bytes 688136 | tf_op jit(solution)/shard_map/ppermute | solution.py:26
  43.5 8.1 %collective-permute-start.5 = (bf16[2,56,1024]{2,1,0:T(8,128)(2,1)S(1)}, bf16[2,56,1024]{2,1,0:T(8,128)(2,1)S(1)}, u32[]{:S(2)}, u32[]{:S(2)}) collective-permute-start(bf16[2,56,1024]{2,1,0:T(8,128)(2,1)S(1)} %collective-permute-done.4), channel_id=1, source_target_pairs={{0,2},{2,4},{4,6},{6,8},{8,10},{10,12},{12,14},{14,16},{16,18},{18... | collective-permute-start | bytes 688136 | tf_op jit(solution)/shard_map/ppermute | solution.py:26
  51.6 8.1 %collective-permute-start.6 = (bf16[2,56,1024]{2,1,0:T(8,128)(2,1)S(1)}, bf16[2,56,1024]{2,1,0:T(8,128)(2,1)S(1)}, u32[]{:S(2)}, u32[]{:S(2)}) collective-permute-start(bf16[2,56,1024]{2,1,0:T(8,128)(2,1)S(1)} %collective-permute-done.5), channel_id=1, source_target_pairs={{0,2},{2,4},{4,6},{6,8},{8,10},{10,12},{12,14},{14,16},{16,18},{18... | collective-permute-start | bytes 688136 | tf_op jit(solution)/shard_map/ppermute | solution.py:26
  59.8 8.1 %collective-permute-start.7 = (bf16[2,56,1024]{2,1,0:T(8,128)(2,1)S(1)}, bf16[2,56,1024]{2,1,0:T(8,128)(2,1)S(1)}, u32[]{:S(2)}, u32[]{:S(2)}) collective-permute-start(bf16[2,56,1024]{2,1,0:T(8,128)(2,1)S(1)} %collective-permute-done.6), channel_id=1, source_target_pairs={{0,2},{2,4},{4,6},{6,8},{8,10},{10,12},{12,14},{14,16},{16,18},{18... | collective-permute-start | bytes 688136 | tf_op jit(solution)/shard_map/ppermute | solution.py:26
  67.9 8.1 %collective-permute-start.8 = (bf16[2,56,1024]{2,1,0:T(8,128)(2,1)S(1)}, bf16[2,56,1024]{2,1,0:T(8,128)(2,1)S(1)}, u32[]{:S(2)}, u32[]{:S(2)}) collective-permute-start(bf16[2,56,1024]{2,1,0:T(8,128)(2,1)S(1)} %collective-permute-done.7), channel_id=1, source_target_pairs={{0,2},{2,4},{4,6},{6,8},{8,10},{10,12},{12,14},{14,16},{16,18},{18... | collective-permute-start | bytes 688136 | tf_op jit(solution)/shard_map/ppermute | solution.py:26
  76.1 8.1 %collective-permute-start.9 = (bf16[2,56,1024]{2,1,0:T(8,128)(2,1)S(1)}, bf16[2,56,1024]{2,1,0:T(8,128)(2,1)S(1)}, u32[]{:S(2)}, u32[]{:S(2)}) collective-permute-start(bf16[2,56,1024]{2,1,0:T(8,128)(2,1)S(1)} %collective-permute-done.8), channel_id=1, source_target_pairs={{0,2},{2,4},{4,6},{6,8},{8,10},{10,12},{12,14},{14,16},{16,18},{18... | collective-permute-start | bytes 688136 | tf_op jit(solution)/shard_map/ppermute | solution.py:26
  84.2 8.1 %collective-permute-start.10 = (bf16[2,56,1024]{2,1,0:T(8,128)(2,1)S(1)}, bf16[2,56,1024]{2,1,0:T(8,128)(2,1)S(1)}, u32[]{:S(2)}, u32[]{:S(2)}) collective-permute-start(bf16[2,56,1024]{2,1,0:T(8,128)(2,1)S(1)} %collective-permute-done.9), channel_id=1, source_target_pairs={{0,2},{2,4},{4,6},{6,8},{8,10},{10,12},{12,14},{14,16},{16,18},{18... | collective-permute-start | bytes 688136 | tf_op jit(solution)/shard_map/ppermute | solution.py:26
  92.3 8.1 %collective-permute-start.11 = (bf16[2,56,1024]{2,1,0:T(8,128)(2,1)S(1)}, bf16[2,56,1024]{2,1,0:T(8,128)(2,1)S(1)}, u32[]{:S(2)}, u32[]{:S(2)}) collective-permute-start(bf16[2,56,1024]{2,1,0:T(8,128)(2,1)S(1)} %collective-permute-done.10), channel_id=1, source_target_pairs={{0,2},{2,4},{4,6},{6,8},{8,10},{10,12},{12,14},{14,16},{16,18},{18... | collective-permute-start | bytes 688136 | tf_op jit(solution)/shard_map/ppermute | solution.py:26
  100.5 8.1 %collective-permute-start.12 = (bf16[2,56,1024]{2,1,0:T(8,128)(2,1)S(1)}, bf16[2,56,1024]{2,1,0:T(8,128)(2,1)S(1)}, u32[]{:S(2)}, u32[]{:S(2)}) collective-permute-start(bf16[2,56,1024]{2,1,0:T(8,128)(2,1)S(1)} %collective-permute-done.11), channel_id=1, source_target_pairs={{0,2},{2,4},{4,6},{6,8},{8,10},{10,12},{12,14},{14,16},{16,18},{18... | collective-permute-start | bytes 688136 | tf_op jit(solution)/shard_map/ppermute | solution.py:26
  108.6 0.7 copy-start.2
  109.3 8.2 %collective-permute-start.13 = (bf16[2,56,1024]{2,1,0:T(8,128)(2,1)S(1)}, bf16[2,56,1024]{2,1,0:T(8,128)(2,1)}, u32[]{:S(2)}, u32[]{:S(2)}) collective-permute-start(bf16[2,56,1024]{2,1,0:T(8,128)(2,1)S(1)} %collective-permute-done.12), channel_id=1, source_target_pairs={{0,2},{2,4},{4,6},{6,8},{8,10},{10,12},{12,14},{14,16},{16,18},{18... | collective-permute-start | bytes 688136 | tf_op jit(solution)/shard_map/ppermute | solution.py:26
  117.5 8.5 %collective-permute-start.14 = (bf16[2,56,1024]{2,1,0:T(8,128)(2,1)}, bf16[2,56,1024]{2,1,0:T(8,128)(2,1)}, u32[]{:S(2)}, u32[]{:S(2)}) collective-permute-start(bf16[2,56,1024]{2,1,0:T(8,128)(2,1)} %collective-permute-done.13), channel_id=1, source_target_pairs={{0,2},{2,4},{4,6},{6,8},{8,10},{10,12},{12,14},{14,16},{16,18},{18... | collective-permute-start | bytes 688136 | tf_op jit(solution)/shard_map/ppermute | solution.py:26
  121.3 9.8 %copy-start.3 = (bf16[2,56,1024]{2,1,0:T(8,128)(2,1)S(1)}, bf16[2,56,1024]{2,1,0:T(8,128)(2,1)}, u32[]{:S(2)}) copy-start(bf16[2,56,1024]{2,1,0:T(8,128)(2,1)} %copy-done.2) | copy-start | bytes 688132
